TPU v7x, 32 devices: a whole 2x2x4 slice. The times are simulated.
32 devices in a mesh: dp: 4 (over x, y), tp: 8 (over z, core).
Axes of the slice: x: 2, y: 2, z: 4, core: 2. Of those that a mesh axis runs over, the one named last changes fastest.
Arguments:
- x: bfloat16 [8192, 3072], P('dp'), parts along dimension 0
- dy: bfloat16 [8192, 3072], P('dp'), parts along dimension 0
- gate: bfloat16 [8192, 8192], P('dp', 'tp'), parts along dimension 0
- up: bfloat16 [8192, 8192], P('dp', 'tp'), parts along dimension 0
- w_gate: bfloat16 [3072, 8192], P(None, 'tp')
- w_up: bfloat16 [3072, 8192], P(None, 'tp')
- w_down: bfloat16 [8192, 3072], P('tp')
Outputs:
- output 1: bfloat16 [8192, 3072], P('dp'), parts along dimension 0
- output 2: bfloat16 [12288, 8192], P('dp', 'tp'), parts along dimension 0
- output 3: bfloat16 [12288, 8192], P('dp', 'tp'), parts along dimension 0
- output 4: bfloat16 [32768, 3072], P(('dp', 'tp')), parts along dimension 0
There are 4 independent parts. A program takes and returns all parts, laid end to end along the dimension named above; an argument that names none is the same for every part.
All inputs are finite; a program needn't handle non-finite values.
Results may differ from a plain program's by a relative error of at most 0.012.
Values are sent between devices in bfloat16 or wider.
A program may use at most 2 GiB of HBM per device.

v0:
```python
import jax
import jax.numpy as jnp
from jax import lax
from jax.sharding import PartitionSpec as P


def act(gate, up):
    return jax.nn.silu(gate) * up


def solution(mesh):
    def step(x, dy, gate, up, w_gate, w_up, w_down):
        hidden, back = jax.vjp(act, gate.astype(jnp.float32), up.astype(jnp.float32))
        d_hidden = jnp.dot(dy, w_down.T, preferred_element_type=jnp.float32)
        d_gate, d_up = (g.astype(jnp.bfloat16) for g in back(d_hidden))
        term = jnp.dot(d_gate, w_gate.T, preferred_element_type=jnp.float32) + jnp.dot(d_up, w_up.T, preferred_element_type=jnp.float32)
        dx = lax.psum(term.astype(jnp.bfloat16), "tp")
        dw_gate = jnp.dot(x.T, d_gate, preferred_element_type=jnp.float32)
        dw_up = jnp.dot(x.T, d_up, preferred_element_type=jnp.float32)
        dw_down = jnp.dot(hidden.astype(jnp.bfloat16).T, dy, preferred_element_type=jnp.float32)
        return dx, *(g.astype(jnp.bfloat16) for g in (dw_gate, dw_up, dw_down))

    tokens, columns, rows = P("dp", None), P(None, "tp"), P("tp", None)
    return jax.shard_map(
        step,
        mesh=mesh,
        in_specs=(tokens, tokens, P("dp", "tp"), P("dp", "tp"), columns, columns, rows),
        out_specs=(tokens, P("dp", "tp"), P("dp", "tp"), P(("dp", "tp"), None)),
        check_vma=False,
    )
```

profile of v0, /device:TPU:0, one launch (start us, length us, event | category | flops | bytes accessed | tf_op | source)
XLA Modules:
  0.0 352.4 jit_solution(4877635843266409278)
XLA Ops:
  7.2 0.0 all-reduce.2.cloned.1.call-start
  7.2 24.7 %fusion.6 = (bf16[2048,1024]{1,0:T(8,128)(2,1)}, f32[2048,1024]{1,0:T(8,128)}) fusion(bf16[2048,1024]{1,0:T(8,128)(2,1)} %param.9, bf16[2048,1024]{1,0:T(8,128)(2,1)} %param.10, bf16[2048,3072]{1,0:T(8,128)(2,1)} %param.8, bf16[1024,3072]{1,0:T(8,128)(2,1)} %param.13), kind=kOutput, calls=%fused_computation.13 | convolution fusion | flops 12912164864 | bytes 39845888 | tf_op jit(solution)/shard_map/dot_general | solution.py:14
  31.9 19.8 %fusion.9 = f32[2048,3072]{1,0:T(8,128)} fusion(bf16[2048,1024]{1,0:T(8,128)(2,1)} %get-tuple-element.8, bf16[3072,1024]{1,0:T(8,128)(2,1)} %param.11), kind=kOutput, calls=%fused_computation.19 | convolution fusion | flops 12884901888 | bytes 35651584 | tf_op jit(solution)/shard_map/dot_general | solution.py:16
  51.7 25.9 %add_convert_fusion = bf16[2048,3072]{1,0:T(8,128)(2,1)} fusion(f32[2048,3072]{1,0:T(8,128)} %fusion.9, bf16[3072,1024]{1,0:T(8,128)(2,1)} %param.12, f32[2048,1024]{1,0:T(8,128)} %get-tuple-element.9, bf16[2048,1024]{1,0:T(8,128)(2,1)} %param.9), kind=kOutput, calls=%fused_computation | convolution fusion | flops 12912164864 | bytes 56623104 | tf_op jit(solution)/shard_map/dot_general | solution.py:16
  77.7 0.0 all-reduce.2.cloned.1.call-update
  77.7 18.6 %convert_bitcast_fusion.1 = bf16[3072,1024]{0,1:T(8,128)(2,1)} fusion(bf16[2048,1024]{1,0:T(8,128)(2,1)} %get-tuple-element.8, bf16[2048,3072]{1,0:T(8,128)(2,1)} %param.7), kind=kOutput, calls=%fused_computation.16 | convolution fusion | flops 12888047616 | bytes 23068672 | tf_op jit(solution)/shard_map/dot_general | solution.py:18
  96.4 8.6 %copy.11 = bf16[3072,1024]{1,0:T(8,128)(2,1)} copy(bf16[3072,1024]{0,1:T(8,128)(2,1)} %convert_bitcast_fusion.1) | data formatting | bytes 12582912
  105.0 22.4 %convert_bitcast_fusion = bf16[3072,1024]{0,1:T(8,128)(2,1)} fusion(bf16[2048,3072]{1,0:T(8,128)(2,1)} %param.7, f32[2048,1024]{1,0:T(8,128)} %get-tuple-element.9, bf16[2048,1024]{1,0:T(8,128)(2,1)} %param.9), kind=kOutput, calls=%fused_computation.15 | convolution fusion | flops 12902727680 | bytes 31457280 | tf_op jit(solution)/shard_map/dot_general | solution.py:19
  127.4 8.6 %copy.12 = bf16[3072,1024]{1,0:T(8,128)(2,1)} copy(bf16[3072,1024]{0,1:T(8,128)(2,1)} %convert_bitcast_fusion) | data formatting | bytes 12582912
  136.0 22.0 %convolution_convert_fusion = bf16[1024,3072]{1,0:T(8,128)(2,1)} fusion(bf16[2048,3072]{1,0:T(8,128)(2,1)} %param.8, bf16[2048,1024]{1,0:T(8,128)(2,1)} %param.10, bf16[2048,1024]{1,0:T(8,128)(2,1)} %param.9), kind=kOutput, calls=%fused_computation.17 | convolution fusion | flops 12904824832 | bytes 27262976 | tf_op jit(solution)/shard_map/dot_general | solution.py:20
  158.0 176.9 %all-reduce.2.cloned.1.call-done = bf16[2048,3072]{1,0:T(8,128)(2,1)} async-done(((bf16[2048,3072]{1,0:T(8,128)(2,1)}), bf16[2048,3072]{1,0:T(8,128)(2,1)}) %all-reduce.2.cloned.1.call-update) | async-done | bytes 12582928 | tf_op jit(solution)/shard_map/psum | solution.py:17
  335.0 10.5 %copy.14 = bf16[2048,3072]{1,0:T(8,128)(2,1)} copy(bf16[2048,3072]{1,0:T(8,128)(2,1)} %all-reduce.2.cloned.1.call-done) | data formatting | bytes 25165824
Async XLA Ops:
  7.2 327.8 %all-reduce.2.cloned.1.call-start = ((), (), s32[]{:S(2)}) async-start(), calls=%async_computation | async-start | bytes 25165824 | tf_op jit(solution)/shard_map/psum | solution.py:17
Sparse Core Ops, SparseCore 0:
  77.8 257.0 all-reduce.1
where the time goes:
time: 353 us; the launch traced here: 352 us
  waiting for transfers between devices  177 us (50%)
  matrix products  134 us (38%)
  local copies, waits for them, and re-layouts  27.8 us (8%)
  between operations  14 us (4%)
    psum x1, waiting for transfers between devices, step(): dx = lax.psum(term.astype(jnp.bfloat16), 'tp')  177 us
    unnamed x3, local copies, waits for them, and re-layouts  27.8 us
    dot_general x1, matrix products, step(): jnp.dot(d_up, w_up.T, preferred_element_type=jnp.float32)  25.9 us
    dot_general x1, matrix products, step(): d_hidden = jnp.dot(dy, w_down.T, preferred_element_type=jnp.float32)  24.7 us
    dot_general x1, matrix products, step(): dw_up = jnp.dot(x.T, d_up, preferred_element_type=jnp.float32)  22.4 us
    dot_general x1, matrix products, step(): jnp.dot(hidden.astype(jnp.bfloat16).T, dy, preferred_element_type=jnp.flo...  22 us
    dot_general x1, matrix products, step(): jnp.dot(d_gate, w_gate.T, preferred_element_type=jnp.float32)  19.8 us
    dot_general x1, matrix products, step(): dw_gate = jnp.dot(x.T, d_gate, preferred_element_type=jnp.float32)  18.6 us
  transfers between devices with their start and end apart: 1, of which 1 were waited for; matrix products, arithmetic and copies ran while one was open for 23% of the time, Pallas kernels for 0%

commit v1 on v0

v1 whole, which is shorter than its diff:
```python
import functools

import jax
import jax.numpy as jnp
from jax import lax
from jax.experimental import pallas as pl
from jax.experimental.pallas import tpu as pltpu
from jax.sharding import PartitionSpec as P

MESH = pl.DeviceIdType.MESH
F32, BF16 = jnp.float32, jnp.bfloat16
ROWS, D, FL = 2048, 3072, 1024
BLK, HALF, CT = 512, 256, 512
NB, NJ = ROWS // BLK, D // CT
NU = NB * NJ
NIN = 4
NT = (((1,), (1,)), ((), ()))
NN = (((1,), (0,)), ((), ()))


def dot(a, b, dims):
    return lax.dot_general(a, b, dims, preferred_element_type=F32)


def m(i, n):
    return pl.multiple_of(i * n, n)


def kernel(comm, x, dy, gate, up, wg, wu, wd, dx, dwg, dwu, dwd,
           wgu_v, wd_v, dgu, hid, dyb, gb, ub, A, B, Q, d_out, d_in,
           w_sem, in_sem, x_sem, y_sem, o_sem, p_sem,
           d_send, d_recv, s1, r1, r2, s3, s4, r4, s5, credit):
    tp = lax.axis_index("tp")
    z, c = tp // 2, lax.rem(tp, 2)
    inner = jnp.logical_and(z >= 1, z <= 2)
    outer = jnp.logical_not(inner)
    sib = z * 2 + (1 - c)
    line = jnp.where(z == 0, 1, jnp.where(z == 1, 0, jnp.where(z == 2, 3, 2))) * 2 + c
    mid = (3 - z) * 2 + c

    def loads(b, pairs):
        out = []
        for h in range(2):
            src = pl.multiple_of(b * BLK + (c if h == 0 else 1 - c) * HALF, HALF)
            rows, dst = pl.ds(src, HALF), pl.ds(h * HALF, HALF)
            for i, src_ref, dst_ref in pairs:
                out.append(pltpu.make_async_copy(src_ref.at[rows, :], dst_ref.at[dst, :], in_sem.at[i + h]))
        return out

    def dy_loads(b):
        return loads(b, [(0, dy, dyb)])

    def gu_loads(b):
        return loads(b, [(2, gate, gb), (4, up, ub)])

    wd_load = pltpu.make_async_copy(wd, wd_v, w_sem.at[0])
    wg_load = pltpu.make_async_copy(wg, wgu_v.at[:, pl.ds(0, FL)], w_sem.at[1])
    wu_load = pltpu.make_async_copy(wu, wgu_v.at[:, pl.ds(FL, FL)], w_sem.at[2])
    for cp in dy_loads(0):
        cp.start()
    wd_load.start()
    for cp in gu_loads(0):
        cp.start()
    wg_load.start()
    wu_load.start()

    if comm:
        barrier = pltpu.get_barrier_semaphore()
        pl.semaphore_signal(barrier, inc=1, device_id={"tp": sib}, device_id_type=MESH)
        pl.semaphore_signal(barrier, inc=1, device_id={"tp": line}, device_id_type=MESH)

        @pl.when(inner)
        def _():
            pl.semaphore_signal(barrier, inc=1, device_id={"tp": mid}, device_id_type=MESH)
            pl.semaphore_wait(barrier, 3)

        @pl.when(outer)
        def _():
            pl.semaphore_wait(barrier, 2)

    def remote(src, dst, send, recv, to):
        return pltpu.make_async_remote_copy(
            src_ref=src, dst_ref=dst, send_sem=send, recv_sem=recv, device_id={"tp": to}, device_id_type=MESH)

    def d_copy(u):
        return remote(d_out.at[lax.rem(u, 2)], d_in.at[lax.rem(u, NIN)], d_send.at[lax.rem(u, 2)],
                      d_recv.at[lax.rem(u, NIN)], sib)

    def p_copy(u):
        return remote(A.at[u], A.at[u], s1.at[u], r1.at[u], line)

    def q_copy(u):
        return remote(A.at[u], Q.at[u], s1.at[u], r2.at[u], mid)

    def piece(u, core):
        b, j = u // NJ, lax.rem(u, NJ)
        return dx.at[pl.ds(pl.multiple_of(b * BLK + core * HALF, HALF), HALF), pl.ds(m(j, CT), CT)]

    def f_copy(u):
        return remote(A.at[u], piece(u, c), s3.at[u], r2.at[u], line)

    def g_copy(u, src):
        return remote(src, piece(u, c), s4.at[u], r4.at[u], sib)

    def l_copy(u):
        return pltpu.make_async_copy(A.at[u], piece(u, c), s5.at[u])

    def when(cond):
        return pl.when(cond)

    def take_sibling(u):
        d_copy(u).wait_recv()

        @when(outer)
        def _():
            A[u] = (B[u] + d_in[lax.rem(u, NIN)].astype(F32)).astype(BF16)
            p_copy(u).start()

        @when(inner)
        def _():
            B[u] = B[u] + d_in[lax.rem(u, NIN)].astype(F32)

        @when(u < NU - NIN)
        def _():
            pl.semaphore_signal(credit, inc=1, device_id={"tp": sib}, device_id_type=MESH)

    def inner_sum(u):
        p_copy(u).wait_recv()
        A[u] = (B[u] + A[u].astype(F32)).astype(BF16)
        q_copy(u).start()

    def final_sum(u):
        q_copy(u).wait_recv()
        q_copy(u).wait_send()
        A[u] = (A[u].astype(F32) + Q[u].astype(F32)).astype(BF16)
        f_copy(u).start()
        g_copy(u, A.at[u]).start()
        l_copy(u).start()

    def forward(u):
        f_copy(u).wait_recv()
        g_copy(u, piece(u, c)).start()

    def tick(h):
        if not comm:
            return

        @when(jnp.logical_and(inner, jnp.logical_and(h >= 2, h < NU + 2)))
        def _():
            inner_sum(h - 2)

        @when(jnp.logical_and(inner, jnp.logical_and(h >= 4, h < NU + 4)))
        def _():
            final_sum(h - 4)

        @when(jnp.logical_and(outer, jnp.logical_and(h >= 6, h < NU + 6)))
        def _():
            forward(h - 6)

    def block(b, _):
        for cp in dy_loads(b):
            cp.wait()

        @when(b == 0)
        def _():
            wd_load.wait()

        for cp in gu_loads(b):
            cp.wait()

        def hidden(n, _):
            cols = pl.ds(m(n, 512), 512)
            dh = dot(dyb[...], wd_v[cols, :], NT)
            g, u = gb[:, cols].astype(F32), ub[:, cols].astype(F32)
            s = jax.nn.sigmoid(g)
            gs = g * s
            rows = pl.ds(m(b, BLK), BLK)
            dgu[rows, cols] = (dh * u * (s * (1.0 + g * (1.0 - s)))).astype(BF16)
            dgu[rows, pl.ds(pl.multiple_of(FL + n * 512, 512), 512)] = (dh * gs).astype(BF16)
            hid[cols, rows] = (gs * u).T.astype(BF16)
            return 0

        lax.fori_loop(0, FL // 512, hidden, 0)

        @when(b < NB - 1)
        def _():
            for cp in dy_loads(b + 1) + gu_loads(b + 1):
                cp.start()

        @when(b == 0)
        def _():
            wg_load.wait()
            wu_load.wait()

        def unit(j, _):
            u = b * NJ + j
            if comm:
                @when(u >= 2)
                def _():
                    d_copy(u - 2).wait_send()
            t = dot(dgu[pl.ds(m(b, BLK), BLK), :], wgu_v[pl.ds(m(j, CT), CT), :], NT)
            B[u] = t[:HALF]
            d_out[lax.rem(u, 2)] = t[HALF:].astype(BF16)
            if comm:
                @when(u >= NIN)
                def _():
                    pl.semaphore_wait(credit, 1)
                d_copy(u).start()

                @when(u >= 1)
                def _():
                    take_sibling(u - 1)

                @when(lax.rem(u, 2) == 1)
                def _():
                    tick(u // 2)
            return 0

        lax.fori_loop(0, NJ, unit, 0)
        return 0

    lax.fori_loop(0, NB, block, 0)
    if comm:
        take_sibling(NU - 1)

    def tile_copies(src, i, slot0, sem):
        slot = lax.rem(i, 2)
        cols = pl.ds(m(i, 512), 512)
        dst_cols = pl.ds(pl.multiple_of((slot0 + slot) * 512, 512), 512)
        return [
            pltpu.make_async_copy(
                src.at[pl.ds(pl.multiple_of(b * BLK + (c if h == 0 else 1 - c) * HALF, HALF), HALF), cols],
                wgu_v.at[pl.ds(b * BLK + h * HALF, HALF), dst_cols],
                sem.at[slot, 2 * b + h],
            )
            for b in range(NB)
            for h in range(2)
        ]

    def gu_out(i):
        slot = lax.rem(i, 2)
        rows = pl.ds(pl.multiple_of(2048 + slot * 512, 512), 512)
        dst = pl.ds(m(i, 512), 512)
        return (
            pltpu.make_async_copy(wgu_v.at[rows, pl.ds(0, FL)], dwg.at[dst, :], o_sem.at[0, slot]),
            pltpu.make_async_copy(wgu_v.at[rows, pl.ds(FL, FL)], dwu.at[dst, :], o_sem.at[1, slot]),
        )

    def down_out(i):
        slot = lax.rem(i, 2)
        return pltpu.make_async_copy(
            wd_v.at[:, pl.ds(m(slot, 512), 512)], dwd.at[:, pl.ds(m(i, 512), 512)], o_sem.at[2, slot])

    for cp in tile_copies(x, 0, 0, x_sem) + tile_copies(dy, 0, 2, y_sem):
        cp.start()
    NI = D // 512
    xt = dyb.at[:, pl.ds(0, ROWS)]

    def grads(i, _):
        slot = lax.rem(i, 2)

        @when(i + 1 < NI)
        def _():
            for cp in tile_copies(x, i + 1, 0, x_sem) + tile_copies(dy, i + 1, 2, y_sem):
                cp.start()

        for cp in tile_copies(x, i, 0, x_sem):
            cp.wait()

        @when(i >= 2)
        def _():
            for cp in gu_out(i - 2):
                cp.wait()
            down_out(i - 2).wait()

        xc = pl.ds(m(slot, 512), 512)

        def flip(r, _):
            rows = pl.ds(m(r, 512), 512)
            xt[:, rows] = wgu_v[rows, xc].T
            return 0

        lax.fori_loop(0, ROWS // 512, flip, 0)
        out_rows = pl.ds(pl.multiple_of(2048 + slot * 512, 512), 512)

        def gu(n, _):
            cols = pl.ds(m(n, 512), 512)
            wgu_v[out_rows, cols] = dot(xt[...], dgu[:, cols], NN).astype(BF16)

            @when(lax.rem(n, 2) == 1)
            def _():
                tick_p(i * 3 + n // 2)
            return 0

        lax.fori_loop(0, 4, gu, 0)
        for cp in gu_out(i):
            cp.start()
        for cp in tile_copies(dy, i, 2, y_sem):
            cp.wait()

        yc = pl.ds(pl.multiple_of((2 + slot) * 512, 512), 512)

        def down(n, _):
            rows = pl.ds(m(n, 512), 512)
            wd_v[rows, pl.ds(m(slot, 512), 512)] = dot(hid[rows, :], wgu_v[pl.ds(0, ROWS), yc], NN).astype(BF16)
            return 0

        lax.fori_loop(0, 2, down, 0)
        down_out(i).start()
        tick_p(i * 3 + 2)
        return 0

    def tick_p(p):
        @when(lax.rem(p, 2) == 1)
        def _():
            tick(NU // 2 + p // 2)

    lax.fori_loop(0, NI, grads, 0)
    for i in (NI - 2, NI - 1):
        for cp in gu_out(i):
            cp.wait()
        down_out(i).wait()

    if comm:
        def drain(h, _):
            tick(h)
            return 0

        lax.fori_loop(NU // 2 + 3 * NI // 2, NU + 6, drain, 0)
        d_copy(NU - 2).wait_send()
        d_copy(NU - 1).wait_send()

        def finish(u, _):
            g_copy(u, A.at[u]).wait()

            @when(outer)
            def _():
                p_copy(u).wait_send()

            @when(inner)
            def _():
                f_copy(u).wait_send()
                l_copy(u).wait()
            return 0

        lax.fori_loop(0, NU, finish, 0)


def fused(comm, *args):
    any_ = pl.BlockSpec(memory_space=pl.ANY)
    V, DMA = pltpu.VMEM, pltpu.SemaphoreType.DMA
    scratch = [
        V((D, 2 * FL), BF16), V((FL, D), BF16), V((ROWS, 2 * FL), BF16), V((FL, ROWS), BF16),
        V((BLK, D), BF16), V((BLK, FL), BF16), V((BLK, FL), BF16),
        V((NU, HALF, CT), BF16), V((NU, HALF, CT), F32), V((NU, HALF, CT), BF16),
        V((2, HALF, CT), BF16), V((NIN, HALF, CT), BF16),
        DMA((3,)), DMA((6,)), DMA((2, 8)), DMA((2, 8)), DMA((3, 2)), DMA((1,)),
        DMA((2,)), DMA((NIN,)), DMA((NU,)), DMA((NU,)), DMA((NU,)), DMA((NU,)), DMA((NU,)), DMA((NU,)), DMA((NU,)),
        pltpu.SemaphoreType.REGULAR,
    ]
    S = jax.ShapeDtypeStruct
    return pl.pallas_call(
        functools.partial(kernel, comm),
        out_shape=(S((ROWS, D), BF16), S((D, FL), BF16), S((D, FL), BF16), S((FL, D), BF16)),
        in_specs=[any_] * 7,
        out_specs=(any_,) * 4,
        scratch_shapes=scratch,
        cost_estimate=pl.CostEstimate(flops=12 * ROWS * D * FL, bytes_accessed=90_000_000, transcendentals=ROWS * FL),
        compiler_params=pltpu.CompilerParams(
            collective_id=0 if comm else None, has_side_effects=True, vmem_limit_bytes=67_043_328),
    )(*args)


def solution(mesh, comm=True):
    tokens, columns, rows = P("dp", None), P(None, "tp"), P("tp", None)
    return jax.shard_map(
        functools.partial(fused, comm),
        mesh=mesh,
        in_specs=(tokens, tokens, P("dp", "tp"), P("dp", "tp"), columns, columns, rows),
        out_specs=(tokens, P("dp", "tp"), P("dp", "tp"), P(("dp", "tp"), None)),
        check_vma=False,
    )
```

time: 353 us -> 201 us (0.57)
  Pallas kernels: 0 us -> 177 us
  waiting for transfers between devices: 177 us -> 0 us
  matrix products: 134 us -> 0 us
  between operations: 14 us -> 0.66 us
  local copies, waits for them, and re-layouts: 27.8 us -> 22.9 us
    pallas_call x0 -> x1, Pallas kernels: none -> 177 us  [fused(): pl.pallas_call(functools.partial(kernel, comm), out_shape=(S((ROWS, D), B...]
    psum x1 -> x0, waiting for transfers between devices: 177 us -> none  [step(): dx = lax.psum(term.astype(jnp.bfloat16), 'tp')]
    dot_general x6 -> x0, matrix products: 134 us -> none  [the longest x1 25.9 us: step(): jnp.dot(d_up, w_up.T, preferred_element_type=jnp.float32)]
    unnamed x3 -> x12, local copies, waits for them, and re-layouts: 27.8 us -> 22.9 us
  transfers between devices with their start and end apart: 1 -> 0, of which waited for: 1 -> 0; matrix products, arithmetic and copies ran while one was open for 23% -> 0% of each run, Pallas kernels for 0% -> 0%
where the time goes in v1:
time: 201 us
  Pallas kernels  177 us (88%)
  local copies, waits for them, and re-layouts  22.9 us (11%)
    pallas_call x1, Pallas kernels, fused(): pl.pallas_call(functools.partial(kernel, comm), out_shape=(S((ROWS, D), B...  177 us
    unnamed x12, local copies, waits for them, and re-layouts  22.9 us

profile of v1, /device:TPU:0, one launch (start us, length us, event | category | flops | bytes accessed | tf_op | source)
XLA Modules:
  0.0 200.5 jit_solution(9178181173134832794)
XLA Ops:
  0.6 177.0 %shard_map.102 = (bf16[2048,3072]{1,0:T(8,128)(2,1)}, bf16[3072,1024]{1,0:T(8,128)(2,1)}, bf16[3072,1024]{1,0:T(8,128)(2,1)}, bf16[1024,3072]{1,0:T(8,128)(2,1)}) custom-call(bf16[2048,3072]{1,0:T(8,128)(2,1)} %x.1, bf16[2048,3072]{1,0:T(8,128)(2,1)} %dy.1, bf16[2048,1024]{1,0:T(8,128)(2,1)} %gate.1, bf16[2048,1024]{1,0:T(8,128)(2,1)} %up.1, ...), custom_call_target="tpu_custom_call" | custom-call | flops 77309411328 | bytes 90000000 | tf_op jit(solution)/shard_map/pallas_call | solution.py:362
  177.6 0.0 copy-start.1
  177.7 11.0 %copy.15 = bf16[2048,3072]{1,0:T(8,128)(2,1)} copy(bf16[2048,3072]{1,0:T(8,128)(2,1)} %get-tuple-element.8) | data formatting | bytes 25165824
  188.7 0.0 copy-done.1
  188.7 0.0 copy-start
  188.7 0.0 slice-start
  188.7 3.2 %copy.16 = bf16[3072,1024]{1,0:T(8,128)(2,1)} copy(bf16[3072,1024]{1,0:T(8,128)(2,1)S(1)} %copy-done.1) | data formatting | bytes 12582912
  191.9 1.9 copy-done
  193.8 0.0 slice-start.1
  193.8 3.1 %copy.17 = bf16[3072,1024]{1,0:T(8,128)(2,1)} copy(bf16[3072,1024]{1,0:T(8,128)(2,1)S(1)} %copy-done) | data formatting | bytes 12582912
  196.8 0.0 slice-done
  196.8 1.0 slice-done.1
  197.8 2.7 %copy.18 = bf16[1024,3072]{1,0:T(8,128)(2,1)} copy(bf16[1024,3072]{1,0:T(8,128)(2,1)S(1)} %bitcast.1) | data formatting | bytes 12582912
  (1 shorter events, 0.0 us)
Async XLA Ops:
  177.6 11.1 %copy-start.1 = (bf16[3072,1024]{1,0:T(8,128)(2,1)S(1)}, bf16[3072,1024]{1,0:T(8,128)(2,1)}, u32[]{:S(2)}) copy-start(bf16[3072,1024]{1,0:T(8,128)(2,1)} %get-tuple-element.9) | copy-start | bytes 18874372
  188.7 5.1 %copy-start = (bf16[3072,1024]{1,0:T(8,128)(2,1)S(1)}, bf16[3072,1024]{1,0:T(8,128)(2,1)}, u32[]{:S(2)}) copy-start(bf16[3072,1024]{1,0:T(8,128)(2,1)} %get-tuple-element.10) | copy-start | bytes 18874372
  188.7 8.1 %slice-start = ((s8[6291456]{0:T(1024)(128)(4,1)}), s8[4194304]{0:T(1024)(128)(4,1)S(1)}, s32[]{:S(2)}) async-start(s8[6291456]{0:T(1024)(128)(4,1)} %bitcast), calls=%async_computation | async-start | bytes 8388608
  193.8 4.1 %slice-start.1 = ((s8[6291456]{0:T(1024)(128)(4,1)}), s8[2097152]{0:T(1024)(128)(4,1)S(1)}, s32[]{:S(2)}) async-start(s8[6291456]{0:T(1024)(128)(4,1)} %bitcast), calls=%async_computation.1 | async-start | bytes 4194304

commit v2 on v1

v2 whole, which is shorter than its diff:
```python
import functools

import jax
import jax.numpy as jnp
from jax import lax
from jax.experimental import pallas as pl
from jax.experimental.pallas import tpu as pltpu
from jax.sharding import PartitionSpec as P

MESH = pl.DeviceIdType.MESH
F32, BF16 = jnp.float32, jnp.bfloat16
ROWS, D, FL = 2048, 3072, 1024
BLK, HALF, TILE, CT = 512, 256, 512, 256
NB, NJ = ROWS // BLK, D // TILE
NT_, NU = NB * NJ, NB * (D // CT)
PER = TILE // CT
NIN, NBUF = 4, 16
NT = (((1,), (1,)), ((), ()))
NN = (((1,), (0,)), ((), ()))


def dot(a, b, dims):
    return lax.dot_general(a, b, dims, preferred_element_type=F32)


def m(i, n):
    return pl.multiple_of(i * n, n)


def kernel(comm, x, dy, gate, up, wg, wu, wd, dx, dwg, dwu, dwd,
           dgu, hid, dyb, gb, ub, xv, yv, B, d_out, d_in,
           w_sem, in_sem, x_sem, y_sem,
           d_send, d_recv, s1, r1, r2, s3, s4, r4, credit, g_credit, f_credit):
    tp = lax.axis_index("tp")
    z, c = tp // 2, lax.rem(tp, 2)
    inner = jnp.logical_and(z >= 1, z <= 2)
    outer = jnp.logical_not(inner)
    sib = z * 2 + (1 - c)
    line = jnp.where(z == 0, 1, jnp.where(z == 1, 0, jnp.where(z == 2, 3, 2))) * 2 + c
    mid = (3 - z) * 2 + c

    def loads(b, pairs):
        out = []
        for h in range(2):
            src = pl.multiple_of(b * BLK + (c if h == 0 else 1 - c) * HALF, HALF)
            rows, dst = pl.ds(src, HALF), pl.ds(h * HALF, HALF)
            for i, src_ref, dst_ref in pairs:
                out.append(pltpu.make_async_copy(src_ref.at[rows, :], dst_ref.at[dst, :], in_sem.at[i + h]))
        return out

    def dy_loads(b):
        return loads(b, [(0, dy, dyb)])

    def gu_loads(b):
        return loads(b, [(2, gate, gb), (4, up, ub)])

    def wd_load(n):
        rows = pl.ds(m(n, 512), 512)
        return pltpu.make_async_copy(wd.at[rows, :], dwd.at[rows, :], w_sem.at[n])

    wg_load = pltpu.make_async_copy(wg, dwg, w_sem.at[2])
    wu_load = pltpu.make_async_copy(wu, dwu, w_sem.at[3])
    for cp in dy_loads(0):
        cp.start()
    wd_load(0).start()
    for cp in gu_loads(0):
        cp.start()
    wd_load(1).start()
    wg_load.start()
    wu_load.start()

    if comm:
        barrier = pltpu.get_barrier_semaphore()
        pl.semaphore_signal(barrier, inc=1, device_id={"tp": sib}, device_id_type=MESH)
        pl.semaphore_signal(barrier, inc=1, device_id={"tp": line}, device_id_type=MESH)

        @pl.when(inner)
        def _():
            pl.semaphore_signal(barrier, inc=1, device_id={"tp": mid}, device_id_type=MESH)
            pl.semaphore_wait(barrier, 3)

        @pl.when(outer)
        def _():
            pl.semaphore_wait(barrier, 2)

    def remote(src, dst, send, recv, to):
        return pltpu.make_async_remote_copy(
            src_ref=src, dst_ref=dst, send_sem=send, recv_sem=recv, device_id={"tp": to}, device_id_type=MESH)

    def at(u, core):
        n = D // CT
        b, j = u // n, lax.rem(u, n)
        return pl.ds(pl.multiple_of(b * BLK + core * HALF, HALF), HALF), pl.ds(m(j, CT), CT)

    def mine(u):
        return dx.at[*at(u, c)]

    def theirs(u):
        return dx.at[*at(u, 1 - c)]

    def d_copy(t):
        return remote(d_out.at[lax.rem(t, 2)], d_in.at[lax.rem(t, NIN)], d_send.at[lax.rem(t, 2)],
                      d_recv.at[lax.rem(t, NIN)], sib)

    def p_copy(u):
        return remote(mine(u), mine(u), s1.at[u], r1.at[u], line)

    def q_copy(u):
        return remote(mine(u), theirs(u), s1.at[u], r2.at[u], mid)

    def f_copy(u):
        return remote(mine(u), mine(u), s3.at[0], r2.at[u], line)

    def g_copy(u):
        return remote(mine(u), mine(u), s4.at[0], r4.at[0], sib)

    def pending(u):
        i = lax.rem(u, PER)
        return lax.rem(u // PER, NBUF), slice(None), pl.ds(m(i, CT), CT)

    def take_sibling(t):
        d_copy(t).wait_recv()
        b, j = t // NJ, lax.rem(t, NJ)
        total = B[lax.rem(t, NBUF)] + d_in[lax.rem(t, NIN)].astype(F32)

        @pl.when(outer)
        def _():
            dx[pl.ds(pl.multiple_of(b * BLK + c * HALF, HALF), HALF), pl.ds(m(j, TILE), TILE)] = total.astype(BF16)
            for i in range(PER):
                p_copy(t * PER + i).start()

        @pl.when(inner)
        def _():
            B[lax.rem(t, NBUF)] = total

        @pl.when(t < NT_ - NIN)
        def _():
            pl.semaphore_signal(credit, inc=1, device_id={"tp": sib}, device_id_type=MESH)

    def inner_sum(u):
        p_copy(u).wait_recv()
        p = at(u, c)
        dx[*p] = (B[*pending(u)] + dx[*p].astype(F32)).astype(BF16)
        q_copy(u).start()

    def final_sum(u):
        q_copy(u).wait_recv()
        q_copy(u).wait_send()
        p = at(u, c)
        dx[*p] = (dx[*p].astype(F32) + dx[*at(u, 1 - c)].astype(F32)).astype(BF16)
        pl.semaphore_signal(g_credit, inc=1, device_id={"tp": sib}, device_id_type=MESH)
        pl.semaphore_wait(f_credit, 1)
        f_copy(u).start()
        pl.semaphore_wait(g_credit, 1)
        g_copy(u).start()

    def release(u):
        p_copy(u).wait_send()
        pl.semaphore_signal(f_credit, inc=1, device_id={"tp": line}, device_id_type=MESH)

    def forward(u):
        f_copy(u).wait_recv()
        g_copy(u).start()

    def tick(h):
        if not comm:
            return

        @pl.when(jnp.logical_and(inner, jnp.logical_and(h >= LAG[0], h < NU + LAG[0])))
        def _():
            inner_sum(h - LAG[0])

        @pl.when(jnp.logical_and(inner, jnp.logical_and(h >= LAG[1], h < NU + LAG[1])))
        def _():
            final_sum(h - LAG[1])

        @pl.when(jnp.logical_and(outer, jnp.logical_and(h >= LAG[0], h < NU + LAG[0])))
        def _():
            release(h - LAG[0])

        @pl.when(jnp.logical_and(outer, jnp.logical_and(h >= LAG[2], h < NU + LAG[2])))
        def _():
            forward(h - LAG[2])

    def block(b, _):
        for cp in dy_loads(b):
            cp.wait()
        rows = pl.ds(m(b, BLK), BLK)

        def hidden(n, _):
            @pl.when(b == 0)
            def _():
                wd_load(n).wait()

            cols = pl.ds(m(n, 512), 512)
            dh = dot(dyb[...], dwd[cols, :], NT)

            @pl.when(n == 0)
            def _():
                for cp in gu_loads(b):
                    cp.wait()

            g, u = gb[:, cols].astype(F32), ub[:, cols].astype(F32)
            s = jax.nn.sigmoid(g)
            gs = g * s
            dgu[rows, cols] = (dh * u * (s * (1.0 + g * (1.0 - s)))).astype(BF16)
            dgu[rows, pl.ds(pl.multiple_of(FL + n * 512, 512), 512)] = (dh * gs).astype(BF16)
            hid[cols, rows] = (gs * u).T.astype(BF16)
            return 0

        lax.fori_loop(0, FL // 512, hidden, 0)

        @pl.when(b < NB - 1)
        def _():
            for cp in dy_loads(b + 1) + gu_loads(b + 1):
                cp.start()

        @pl.when(b == 0)
        def _():
            wg_load.wait()
            wu_load.wait()

        def tile(j, _):
            t = b * NJ + j
            if comm:
                @pl.when(t >= 2)
                def _():
                    d_copy(t - 2).wait_send()
            cols = pl.ds(m(j, TILE), TILE)
            v = dot(dgu[rows, pl.ds(0, FL)], dwg[cols, :], NT) + dot(dgu[rows, pl.ds(FL, FL)], dwu[cols, :], NT)
            B[lax.rem(t, NBUF)] = v[:HALF]
            d_out[lax.rem(t, 2)] = v[HALF:].astype(BF16)
            if comm:
                @pl.when(t >= NIN)
                def _():
                    pl.semaphore_wait(credit, 1)
                d_copy(t).start()

                @pl.when(t >= 1)
                def _():
                    take_sibling(t - 1)

                tick(t)
            return 0

        lax.fori_loop(0, NJ, tile, 0)
        return 0

    def tile_copies(src, dst, i, sem):
        cols = pl.ds(m(i, 512), 512)
        return [
            pltpu.make_async_copy(
                src.at[pl.ds(pl.multiple_of(b * BLK + (c if h == 0 else 1 - c) * HALF, HALF), HALF), cols],
                dst.at[pl.ds(b * BLK + h * HALF, HALF), :],
                sem.at[2 * b + h],
            )
            for b in range(NB)
            for h in range(2)
        ]

    for cp in tile_copies(x, xv, 0, x_sem) + tile_copies(dy, yv, 0, y_sem):
        cp.start()

    lax.fori_loop(0, NB, block, 0)
    if comm:
        take_sibling(NT_ - 1)

    NI = D // 512
    xt = dyb.at[:, pl.ds(0, ROWS)]

    def grads(i, _):
        for cp in tile_copies(x, xv, i, x_sem):
            cp.wait()

        def flip(r, _):
            rows = pl.ds(m(r, 512), 512)
            xt[:, rows] = xv[rows, :].T
            return 0

        lax.fori_loop(0, ROWS // 512, flip, 0)

        @pl.when(i + 1 < NI)
        def _():
            for cp in tile_copies(x, xv, i + 1, x_sem):
                cp.start()

        out = pl.ds(m(i, 512), 512)

        def gu(n, _):
            cols = pl.ds(m(n, 512), 512)
            dwg[out, cols] = dot(xt[...], dgu[:, cols], NN).astype(BF16)
            dwu[out, cols] = dot(xt[...], dgu[:, pl.ds(pl.multiple_of(FL + n * 512, 512), 512)], NN).astype(BF16)
            tick(NT_ + 4 * i + n)
            return 0

        lax.fori_loop(0, 2, gu, 0)
        for cp in tile_copies(dy, yv, i, y_sem):
            cp.wait()

        def down(n, _):
            rows = pl.ds(m(n, 512), 512)
            dwd[rows, out] = dot(hid[rows, :], yv[...], NN).astype(BF16)
            tick(NT_ + 4 * i + 2 + n)
            return 0

        lax.fori_loop(0, 2, down, 0)

        @pl.when(i + 1 < NI)
        def _():
            for cp in tile_copies(dy, yv, i + 1, y_sem):
                cp.start()
        return 0

    lax.fori_loop(0, NI, grads, 0)

    if comm:
        def drain(h, _):
            tick(h)
            return 0

        lax.fori_loop(NT_ + 4 * NI, NU + LAG[2], drain, 0)
        d_copy(NT_ - 2).wait_send()
        d_copy(NT_ - 1).wait_send()
        half = dx.at[pl.ds(0, ROWS // 2), :]
        remote(half, half, s4.at[0], r4.at[0], sib).wait()

        @pl.when(inner)
        def _():
            remote(half, half, s3.at[0], r2.at[0], line).wait_send()


def write(*refs):
    n = len(refs) // 2
    sem, refs = refs[-1], refs[:-1]
    copies = []
    for i in range(n):
        src, dst = refs[i], refs[n + i]
        rows = src.shape[0] // 4
        for k in range(4):
            part = pl.ds(k * rows, rows)
            copies.append(pltpu.make_async_copy(src.at[part, :], dst.at[part, :], sem.at[i, k]))
    for cp in copies:
        cp.start()
    for cp in copies:
        cp.wait()


SHAPES = ((ROWS, D), (D, FL), (D, FL), (FL, D))
LAG = (3, 5, 7)


def fused(comm, *args):
    any_, vmem = pl.BlockSpec(memory_space=pl.ANY), pl.BlockSpec(memory_space=pltpu.VMEM)
    V, DMA = pltpu.VMEM, pltpu.SemaphoreType.DMA
    scratch = [
        V((ROWS, 2 * FL), BF16), V((FL, ROWS), BF16),
        V((BLK, D), BF16), V((BLK, FL), BF16), V((BLK, FL), BF16), V((ROWS, 512), BF16), V((ROWS, 512), BF16),
        V((NBUF, HALF, TILE), F32), V((2, HALF, TILE), BF16), V((NIN, HALF, TILE), BF16),
        DMA((4,)), DMA((6,)), DMA((8,)), DMA((8,)),
        DMA((2,)), DMA((NIN,)), DMA((NU,)), DMA((NU,)), DMA((NU,)), DMA((1,)), DMA((1,)), DMA((1,)),
        pltpu.SemaphoreType.REGULAR, pltpu.SemaphoreType.REGULAR, pltpu.SemaphoreType.REGULAR,
    ]
    held = pl.pallas_call(
        functools.partial(kernel, comm),
        out_shape=tuple(pltpu.VMEM(s, BF16) for s in SHAPES),
        in_specs=[any_] * 7,
        out_specs=(vmem,) * 4,
        scratch_shapes=scratch,
        cost_estimate=pl.CostEstimate(flops=12 * ROWS * D * FL, bytes_accessed=90_000_000, transcendentals=ROWS * FL),
        compiler_params=pltpu.CompilerParams(
            collective_id=0 if comm else None, has_side_effects=True, vmem_limit_bytes=VLIM),
    )(*args)
    return pl.pallas_call(
        write,
        out_shape=tuple(jax.ShapeDtypeStruct(s, BF16) for s in SHAPES),
        in_specs=[vmem] * 4,
        out_specs=(any_,) * 4,
        scratch_shapes=[DMA((4, 4))],
        compiler_params=pltpu.CompilerParams(vmem_limit_bytes=1 << 20),
    )(*held)


VLIM = (64 << 20) - (64 << 10) - 2 * ROWS * D - 6 * D * FL


def solution(mesh, comm=True):
    tokens, columns, rows = P("dp", None), P(None, "tp"), P("tp", None)
    return jax.shard_map(
        functools.partial(fused, comm),
        mesh=mesh,
        in_specs=(tokens, tokens, P("dp", "tp"), P("dp", "tp"), columns, columns, rows),
        out_specs=(tokens, P("dp", "tp"), P("dp", "tp"), P(("dp", "tp"), None)),
        check_vma=False,
    )
```

time: 201 us -> 189 us (0.940)
  local copies, waits for them, and re-layouts: 22.9 us -> 0 us
  Pallas kernels: 177 us -> 189 us
    unnamed x12 -> x0, local copies, waits for them, and re-layouts: 22.9 us -> none
    pallas_call x1 -> x2, Pallas kernels: 177 us -> 189 us  [the longest x1 178 us: fused(): pl.pallas_call(functools.partial(kernel, comm), out_shape=tuple((pltpu.VM...]
where the time goes in v2:
time: 189 us
  Pallas kernels  189 us (100%)
    pallas_call x1, Pallas kernels, fused(): pl.pallas_call(functools.partial(kernel, comm), out_shape=tuple((pltpu.VM...  178 us
    pallas_call x1, Pallas kernels, fused(): pl.pallas_call(write, out_shape=tuple((jax.ShapeDtypeStruct(s, BF16) for...  10.4 us

profile of v2, /device:TPU:0, one launch (start us, length us, event | category | flops | bytes accessed | tf_op | source)
XLA Modules:
  0.0 189.2 jit_solution(17373403433107771478)
XLA Ops:
  0.6 178.1 %shard_map.102 = (bf16[2048,3072]{1,0:T(8,128)(2,1)S(1)}, bf16[3072,1024]{1,0:T(8,128)(2,1)S(1)}, bf16[3072,1024]{1,0:T(8,128)(2,1)S(1)}, bf16[1024,3072]{1,0:T(8,128)(2,1)S(1)}) custom-call(bf16[2048,3072]{1,0:T(8,128)(2,1)} %x.1, bf16[2048,3072]{1,0:T(8,128)(2,1)} %dy.1, bf16[2048,1024]{1,0:T(8,128)(2,1)} %gate.1, bf16[2048,1024]{1,0:T(8,128)(2,1)} %up.1, ...), custom_call_target="tpu_custom_call" | custom-call | flops 77309411328 | bytes 90000000 | tf_op jit(solution)/shard_map/pallas_call | solution.py:363
  178.8 10.4 %shard_map.103 = (bf16[2048,3072]{1,0:T(8,128)(2,1)}, bf16[3072,1024]{1,0:T(8,128)(2,1)}, bf16[3072,1024]{1,0:T(8,128)(2,1)}, bf16[1024,3072]{1,0:T(8,128)(2,1)}) custom-call(bf16[2048,3072]{1,0:T(8,128)(2,1)S(1)} %get-tuple-element.8.refs_0_, bf16[3072,1024]{1,0:T(8,128)(2,1)S(1)} %get-tuple-element.9.refs_1_, ...), custom_call_target="tpu_custom_call" | custom-call | tf_op jit(solution)/shard_map/pallas_call | solution.py:373

commit v3 on v2

--- a/solution.py
+++ b/solution.py
@@ -14,7 +14,7 @@
 NB, NJ = ROWS // BLK, D // TILE
 NT_, NU = NB * NJ, NB * (D // CT)
 PER = TILE // CT
-NIN, NBUF = 4, 16
+NIN, NBUF = 4, 14
 NT = (((1,), (1,)), ((), ()))
 NN = (((1,), (0,)), ((), ()))
 
@@ -60,14 +60,8 @@
 
     wg_load = pltpu.make_async_copy(wg, dwg, w_sem.at[2])
     wu_load = pltpu.make_async_copy(wu, dwu, w_sem.at[3])
-    for cp in dy_loads(0):
+    for cp in dy_loads(0) + [wd_load(0)] + gu_loads(0):
         cp.start()
-    wd_load(0).start()
-    for cp in gu_loads(0):
-        cp.start()
-    wd_load(1).start()
-    wg_load.start()
-    wu_load.start()
 
     if comm:
         barrier = pltpu.get_barrier_semaphore()
@@ -182,6 +176,18 @@
         def _():
             forward(h - LAG[2])
 
+    def tile_copies(src, dst, i, sem):
+        cols = pl.ds(m(i, 512), 512)
+        return [
+            pltpu.make_async_copy(
+                src.at[pl.ds(pl.multiple_of(b * BLK + (c if h == 0 else 1 - c) * HALF, HALF), HALF), cols],
+                dst.at[pl.ds(b * BLK + h * HALF, HALF), :],
+                sem.at[2 * b + h],
+            )
+            for b in range(NB)
+            for h in range(2)
+        ]
+
     def block(b, _):
         for cp in dy_loads(b):
             cp.wait()
@@ -191,6 +197,12 @@
             @pl.when(b == 0)
             def _():
                 wd_load(n).wait()
+
+                @pl.when(n == 0)
+                def _():
+                    wd_load(1).start()
+                    wg_load.start()
+                    wu_load.start()
 
             cols = pl.ds(m(n, 512), 512)
             dh = dot(dyb[...], dwd[cols, :], NT)
@@ -206,6 +218,7 @@
             dgu[rows, cols] = (dh * u * (s * (1.0 + g * (1.0 - s)))).astype(BF16)
             dgu[rows, pl.ds(pl.multiple_of(FL + n * 512, 512), 512)] = (dh * gs).astype(BF16)
             hid[cols, rows] = (gs * u).T.astype(BF16)
+            tick(8 * b + n)
             return 0
 
         lax.fori_loop(0, FL // 512, hidden, 0)
@@ -219,6 +232,8 @@
         def _():
             wg_load.wait()
             wu_load.wait()
+            for cp in tile_copies(x, xv, 0, x_sem) + tile_copies(dy, yv, 0, y_sem):
+                cp.start()
 
         def tile(j, _):
             t = b * NJ + j
@@ -240,26 +255,11 @@
                 def _():
                     take_sibling(t - 1)
 
-                tick(t)
+                tick(8 * b + 2 + j)
             return 0
 
         lax.fori_loop(0, NJ, tile, 0)
         return 0
-
-    def tile_copies(src, dst, i, sem):
-        cols = pl.ds(m(i, 512), 512)
-        return [
-            pltpu.make_async_copy(
-                src.at[pl.ds(pl.multiple_of(b * BLK + (c if h == 0 else 1 - c) * HALF, HALF), HALF), cols],
-                dst.at[pl.ds(b * BLK + h * HALF, HALF), :],
-                sem.at[2 * b + h],
-            )
-            for b in range(NB)
-            for h in range(2)
-        ]
-
-    for cp in tile_copies(x, xv, 0, x_sem) + tile_copies(dy, yv, 0, y_sem):
-        cp.start()
 
     lax.fori_loop(0, NB, block, 0)
     if comm:
@@ -278,6 +278,7 @@
             return 0
 
         lax.fori_loop(0, ROWS // 512, flip, 0)
+        tick(8 * NB + 4 * i)
 
         @pl.when(i + 1 < NI)
         def _():
@@ -290,7 +291,7 @@
             cols = pl.ds(m(n, 512), 512)
             dwg[out, cols] = dot(xt[...], dgu[:, cols], NN).astype(BF16)
             dwu[out, cols] = dot(xt[...], dgu[:, pl.ds(pl.multiple_of(FL + n * 512, 512), 512)], NN).astype(BF16)
-            tick(NT_ + 4 * i + n)
+            tick(8 * NB + 4 * i + 1 + n)
             return 0
 
         lax.fori_loop(0, 2, gu, 0)
@@ -300,10 +301,10 @@
         def down(n, _):
             rows = pl.ds(m(n, 512), 512)
             dwd[rows, out] = dot(hid[rows, :], yv[...], NN).astype(BF16)
-            tick(NT_ + 4 * i + 2 + n)
             return 0
 
         lax.fori_loop(0, 2, down, 0)
+        tick(8 * NB + 4 * i + 3)
 
         @pl.when(i + 1 < NI)
         def _():
@@ -318,7 +319,7 @@
             tick(h)
             return 0
 
-        lax.fori_loop(NT_ + 4 * NI, NU + LAG[2], drain, 0)
+        lax.fori_loop(8 * NB + 4 * NI, NU + LAG[2], drain, 0)
         d_copy(NT_ - 2).wait_send()
         d_copy(NT_ - 1).wait_send()
         half = dx.at[pl.ds(0, ROWS // 2), :]
@@ -346,7 +347,7 @@
 
 
 SHAPES = ((ROWS, D), (D, FL), (D, FL), (FL, D))
-LAG = (3, 5, 7)
+LAG = (5, 7, 9)
 
 
 def fused(comm, *args):

time: 189 us -> 176 us (0.931)
  Pallas kernels: 189 us -> 176 us
    pallas_call x1, Pallas kernels: 178 us -> 165 us  [fused(): pl.pallas_call(functools.partial(kernel, comm), out_shape=tuple((pltpu.VM...]
where the time goes in v3:
time: 176 us
  Pallas kernels  176 us (100%)
    pallas_call x1, Pallas kernels, fused(): pl.pallas_call(functools.partial(kernel, comm), out_shape=tuple((pltpu.VM...  165 us
    pallas_call x1, Pallas kernels, fused(): pl.pallas_call(write, out_shape=tuple((jax.ShapeDtypeStruct(s, BF16) for...  10.4 us

profile of v3, /device:TPU:0, one launch (start us, length us, event | category | flops | bytes accessed | tf_op | source)
XLA Modules:
  0.0 176.3 jit_solution(5342255206272181797)
XLA Ops:
  0.6 165.2 %shard_map.102 = (bf16[2048,3072]{1,0:T(8,128)(2,1)S(1)}, bf16[3072,1024]{1,0:T(8,128)(2,1)S(1)}, bf16[3072,1024]{1,0:T(8,128)(2,1)S(1)}, bf16[1024,3072]{1,0:T(8,128)(2,1)S(1)}) custom-call(bf16[2048,3072]{1,0:T(8,128)(2,1)} %x.1, bf16[2048,3072]{1,0:T(8,128)(2,1)} %dy.1, bf16[2048,1024]{1,0:T(8,128)(2,1)} %gate.1, bf16[2048,1024]{1,0:T(8,128)(2,1)} %up.1, ...), custom_call_target="tpu_custom_call" | custom-call | flops 77309411328 | bytes 90000000 | tf_op jit(solution)/shard_map/pallas_call | solution.py:364
  165.8 10.4 %shard_map.103 = (bf16[2048,3072]{1,0:T(8,128)(2,1)}, bf16[3072,1024]{1,0:T(8,128)(2,1)}, bf16[3072,1024]{1,0:T(8,128)(2,1)}, bf16[1024,3072]{1,0:T(8,128)(2,1)}) custom-call(bf16[2048,3072]{1,0:T(8,128)(2,1)S(1)} %get-tuple-element.8.refs_0_, bf16[3072,1024]{1,0:T(8,128)(2,1)S(1)} %get-tuple-element.9.refs_1_, ...), custom_call_target="tpu_custom_call" | custom-call | tf_op jit(solution)/shard_map/pallas_call | solution.py:374

commit v4 on v3

--- a/solution.py
+++ b/solution.py
@@ -14,7 +14,7 @@
 NB, NJ = ROWS // BLK, D // TILE
 NT_, NU = NB * NJ, NB * (D // CT)
 PER = TILE // CT
-NIN, NBUF = 4, 14
+NIN, NBUF = 4, 11
 NT = (((1,), (1,)), ((), ()))
 NN = (((1,), (0,)), ((), ()))
 
@@ -29,7 +29,7 @@
 
 def kernel(comm, x, dy, gate, up, wg, wu, wd, dx, dwg, dwu, dwd,
            dgu, hid, dyb, gb, ub, xv, yv, B, d_out, d_in,
-           w_sem, in_sem, x_sem, y_sem,
+           w_sem, k_sem, in_sem, x_sem, y_sem,
            d_send, d_recv, s1, r1, r2, s3, s4, r4, credit, g_credit, f_credit):
     tp = lax.axis_index("tp")
     z, c = tp // 2, lax.rem(tp, 2)
@@ -51,6 +51,14 @@
     def dy_loads(b):
         return loads(b, [(0, dy, dyb)])
 
+    def first_loads(k):
+        cols = pl.ds(k * (D // 2), D // 2)
+        out = [pltpu.make_async_copy(wd.at[pl.ds(0, 512), cols], dwd.at[pl.ds(0, 512), cols], k_sem.at[k, 2])]
+        for h in range(2):
+            src = pl.ds(pl.multiple_of((c if h == 0 else 1 - c) * HALF, HALF), HALF)
+            out.append(pltpu.make_async_copy(dy.at[src, cols], dyb.at[pl.ds(h * HALF, HALF), cols], k_sem.at[k, h]))
+        return out
+
     def gu_loads(b):
         return loads(b, [(2, gate, gb), (4, up, ub)])
 
@@ -60,7 +68,7 @@
 
     wg_load = pltpu.make_async_copy(wg, dwg, w_sem.at[2])
     wu_load = pltpu.make_async_copy(wu, dwu, w_sem.at[3])
-    for cp in dy_loads(0) + [wd_load(0)] + gu_loads(0):
+    for cp in first_loads(0) + first_loads(1) + gu_loads(0):
         cp.start()
 
     if comm:
@@ -71,6 +79,10 @@
         @pl.when(inner)
         def _():
             pl.semaphore_signal(barrier, inc=1, device_id={"tp": mid}, device_id_type=MESH)
+
+    def enter():
+        @pl.when(inner)
+        def _():
             pl.semaphore_wait(barrier, 3)
 
         @pl.when(outer)
@@ -160,13 +172,13 @@
         if not comm:
             return
 
+        @pl.when(jnp.logical_and(inner, jnp.logical_and(h >= LAG[1], h < NU + LAG[1])))
+        def _():
+            final_sum(h - LAG[1])
+
         @pl.when(jnp.logical_and(inner, jnp.logical_and(h >= LAG[0], h < NU + LAG[0])))
         def _():
             inner_sum(h - LAG[0])
-
-        @pl.when(jnp.logical_and(inner, jnp.logical_and(h >= LAG[1], h < NU + LAG[1])))
-        def _():
-            final_sum(h - LAG[1])
 
         @pl.when(jnp.logical_and(outer, jnp.logical_and(h >= LAG[0], h < NU + LAG[0])))
         def _():
@@ -188,40 +200,29 @@
             for h in range(2)
         ]
 
+    def hidden(b, n, dh):
+        cols, rows = pl.ds(m(n, 512), 512), pl.ds(m(b, BLK), BLK)
+        g, u = gb[:, cols].astype(F32), ub[:, cols].astype(F32)
+        s = jax.nn.sigmoid(g)
+        gs = g * s
+        dgu[rows, cols] = (dh * u * (s * (1.0 + g * (1.0 - s)))).astype(BF16)
+        dgu[rows, pl.ds(pl.multiple_of(FL + n * 512, 512), 512)] = (dh * gs).astype(BF16)
+        hid[cols, rows] = (gs * u).T.astype(BF16)
+
     def block(b, _):
-        for cp in dy_loads(b):
-            cp.wait()
         rows = pl.ds(m(b, BLK), BLK)
 
-        def hidden(n, _):
-            @pl.when(b == 0)
-            def _():
-                wd_load(n).wait()
-
-                @pl.when(n == 0)
-                def _():
-                    wd_load(1).start()
-                    wg_load.start()
-                    wu_load.start()
-
-            cols = pl.ds(m(n, 512), 512)
-            dh = dot(dyb[...], dwd[cols, :], NT)
-
-            @pl.when(n == 0)
-            def _():
-                for cp in gu_loads(b):
-                    cp.wait()
-
-            g, u = gb[:, cols].astype(F32), ub[:, cols].astype(F32)
-            s = jax.nn.sigmoid(g)
-            gs = g * s
-            dgu[rows, cols] = (dh * u * (s * (1.0 + g * (1.0 - s)))).astype(BF16)
-            dgu[rows, pl.ds(pl.multiple_of(FL + n * 512, 512), 512)] = (dh * gs).astype(BF16)
-            hid[cols, rows] = (gs * u).T.astype(BF16)
-            tick(8 * b + n)
-            return 0
-
-        lax.fori_loop(0, FL // 512, hidden, 0)
+        @pl.when(b > 0)
+        def _():
+            for cp in dy_loads(b) + gu_loads(b):
+                cp.wait()
+
+            def step(n, _):
+                hidden(b, n, dot(dyb[...], dwd[pl.ds(m(n, 512), 512), :], NT))
+                tick(8 * b + n)
+                return 0
+
+            lax.fori_loop(0, FL // 512, step, 0)
 
         @pl.when(b < NB - 1)
         def _():
@@ -261,6 +262,32 @@
         lax.fori_loop(0, NJ, tile, 0)
         return 0
 
+    for cp in first_loads(0):
+        cp.wait()
+    wd_load(1).start()
+    wg_load.start()
+    wu_load.start()
+    lo, hi = pl.ds(0, D // 2), pl.ds(D // 2, D // 2)
+
+    def first(n, _):
+        @pl.when(n == 1)
+        def _():
+            wd_load(1).wait()
+
+        rows = pl.ds(m(n, 512), 512)
+        dh = dot(dyb[:, lo], dwd[rows, lo], NT)
+
+        @pl.when(n == 0)
+        def _():
+            for cp in first_loads(1) + gu_loads(0):
+                cp.wait()
+
+        hidden(0, n, dh + dot(dyb[:, hi], dwd[rows, hi], NT))
+        return 0
+
+    lax.fori_loop(0, FL // 512, first, 0)
+    if comm:
+        enter()
     lax.fori_loop(0, NB, block, 0)
     if comm:
         take_sibling(NT_ - 1)
@@ -357,7 +384,7 @@
         V((ROWS, 2 * FL), BF16), V((FL, ROWS), BF16),
         V((BLK, D), BF16), V((BLK, FL), BF16), V((BLK, FL), BF16), V((ROWS, 512), BF16), V((ROWS, 512), BF16),
         V((NBUF, HALF, TILE), F32), V((2, HALF, TILE), BF16), V((NIN, HALF, TILE), BF16),
-        DMA((4,)), DMA((6,)), DMA((8,)), DMA((8,)),
+        DMA((4,)), DMA((2, 3)), DMA((6,)), DMA((8,)), DMA((8,)),
         DMA((2,)), DMA((NIN,)), DMA((NU,)), DMA((NU,)), DMA((NU,)), DMA((1,)), DMA((1,)), DMA((1,)),
         pltpu.SemaphoreType.REGULAR, pltpu.SemaphoreType.REGULAR, pltpu.SemaphoreType.REGULAR,
     ]

time: 176 us -> 176 us (level)
  no operation moved by 1% of the time
where the time goes in v4:
time: 176 us
  Pallas kernels  175 us (99%)
    pallas_call x1, Pallas kernels, fused(): pl.pallas_call(functools.partial(kernel, comm), out_shape=tuple((pltpu.VM...  164 us
    pallas_call x1, Pallas kernels, fused(): pl.pallas_call(write, out_shape=tuple((jax.ShapeDtypeStruct(s, BF16) for...  10.4 us

profile of v4, /device:TPU:0, one launch (start us, length us, event | category | flops | bytes accessed | tf_op | source)
XLA Modules:
  0.0 175.5 jit_solution(14981380261793942636)
XLA Ops:
  0.6 164.4 %shard_map.102 = (bf16[2048,3072]{1,0:T(8,128)(2,1)S(1)}, bf16[3072,1024]{1,0:T(8,128)(2,1)S(1)}, bf16[3072,1024]{1,0:T(8,128)(2,1)S(1)}, bf16[1024,3072]{1,0:T(8,128)(2,1)S(1)}) custom-call(bf16[2048,3072]{1,0:T(8,128)(2,1)} %x.1, bf16[2048,3072]{1,0:T(8,128)(2,1)} %dy.1, bf16[2048,1024]{1,0:T(8,128)(2,1)} %gate.1, bf16[2048,1024]{1,0:T(8,128)(2,1)} %up.1, ...), custom_call_target="tpu_custom_call" | custom-call | flops 77309411328 | bytes 90000000 | tf_op jit(solution)/shard_map/pallas_call | solution.py:391
  165.1 10.4 %shard_map.103 = (bf16[2048,3072]{1,0:T(8,128)(2,1)}, bf16[3072,1024]{1,0:T(8,128)(2,1)}, bf16[3072,1024]{1,0:T(8,128)(2,1)}, bf16[1024,3072]{1,0:T(8,128)(2,1)}) custom-call(bf16[2048,3072]{1,0:T(8,128)(2,1)S(1)} %get-tuple-element.8.refs_0_, bf16[3072,1024]{1,0:T(8,128)(2,1)S(1)} %get-tuple-element.9.refs_1_, ...), custom_call_target="tpu_custom_call" | custom-call | tf_op jit(solution)/shard_map/pallas_call | solution.py:401
